TPU v7x, 32 devices: a whole 2x2x4 slice. The times are simulated.
32 devices in a mesh: dp: 4 (over y, x), seq: 4 (over z), grp: 2 (over core).
Axes of the slice: x: 2, y: 2, z: 4, core: 2. Of those that a mesh axis runs over, the one named last changes fastest.
Arguments:
- text_proj: bfloat16 [3, 16, 12, 128, 128], P(None, 'dp', None, ('seq', 'grp')), may hold values from -50 to 50
- image_proj: bfloat16 [3, 16, 12, 160, 128], P(None, ('dp', 'seq'), None, 'grp'), may hold values from -50 to 50
- text_grad: bfloat16 [16, 12, 128, 128], P('dp', None, ('seq', 'grp')), may hold values from -15 to 15
- image_grad: bfloat16 [16, 12, 160, 128], P(('dp', 'seq'), None, 'grp'), may hold values from -15 to 15
- text_lengths: int32 [16], P(('dp', 'seq')), may hold values from 1 to 128
- norm_gains: float32 [2, 2, 128], replicated, may hold values from 0.7 to 5.2
Outputs:
- text_out: bfloat16 [16, 12, 128, 128], P('dp', None, ('seq', 'grp'))
- image_out: bfloat16 [16, 12, 160, 128], P(('dp', 'seq'), None, 'grp')
- text_proj_grad: bfloat16 [3, 16, 12, 128, 128], P(None, 'dp', None, ('seq', 'grp'))
- image_proj_grad: bfloat16 [3, 16, 12, 160, 128], P(None, ('dp', 'seq'), None, 'grp')
- gain_grad: float32 [2, 2, 128], replicated
All inputs are finite; a program needn't handle non-finite values.
Results may differ from a plain program's by a relative error of at most 0.025.
The roundings to bfloat16 on the way count: a program that leaves them out, or rounds other values in their place, can miss the bound.
Values may be sent and summed in bfloat16 or wider, within the bound.
No kernel may reach another device: no remote copies, remote signals or barrier semaphores. Data moves between devices by JAX's collectives and lax.ppermute only.
A program may use at most 64 MiB of HBM per device.

v0:
```python
import jax
import jax.numpy as jnp
from jax import lax
from jax.sharding import PartitionSpec as P

TXT = 128
EPSILON = 1e-06
MASKED = -1e30


def forward(queries, key_rows, value_rows, key_valid):
    factor = queries.shape[-1] ** (-0.5)
    scores = (
        jnp.einsum("nqd,nkd->nqk", queries, key_rows, preferred_element_type=jnp.float32) * factor
    )
    scores = jnp.where(key_valid[:, None, :], scores, MASKED)
    row_max = jnp.max(scores, axis=-1, keepdims=True)
    exponent = jnp.exp(scores - row_max)
    attn_probs = exponent / jnp.sum(exponent, axis=-1, keepdims=True)
    rounded_probs = attn_probs.astype(jnp.bfloat16)
    attn_local = jnp.einsum(
        "nqk,nkd->nqd", rounded_probs, value_rows, preferred_element_type=jnp.float32
    )
    return (attn_probs, rounded_probs, attn_local)


def backward_terms(queries, key_rows, value_rows, attn_probs, rounded_probs, grad_out):
    factor = queries.shape[-1] ** (-0.5)
    grad_value = jnp.einsum(
        "nqk,nqd->nkd", rounded_probs, grad_out, preferred_element_type=jnp.float32
    )
    grad_probs = jnp.einsum(
        "nqd,nkd->nqk", grad_out, value_rows, preferred_element_type=jnp.float32
    )
    row_delta = jnp.sum(attn_probs * grad_probs, axis=-1, keepdims=True)
    grad_scores = (attn_probs * (grad_probs - row_delta) * factor).astype(jnp.bfloat16)
    grad_query = jnp.einsum(
        "nqk,nkd->nqd", grad_scores, key_rows, preferred_element_type=jnp.float32
    ).astype(jnp.bfloat16)
    grad_key = jnp.einsum("nqk,nqd->nkd", grad_scores, queries, preferred_element_type=jnp.float32)
    return (grad_query, grad_key, grad_value)


def sums_item(packed):
    query_one, key_one, value_one, valid_one, grad_one = packed
    attn_probs, rounded_probs, attn_local = forward(
        query_one[None], key_one[None], value_one[None], valid_one[None]
    )
    grad_query, grad_key, grad_value = backward_terms(
        query_one[None], key_one[None], value_one[None], attn_probs, rounded_probs, grad_one[None]
    )
    return (attn_local[0].astype(jnp.bfloat16), grad_query[0], grad_key[0], grad_value[0])


def whole_item(packed):
    attn_local, grad_query, grad_key, grad_value = sums_item(packed)
    return (attn_local, grad_query, grad_key.astype(jnp.bfloat16), grad_value.astype(jnp.bfloat16))


def unit_parts(raw_bf):
    raw_vals = raw_bf.astype(jnp.float32)
    inverse = lax.rsqrt(jnp.mean(raw_vals * raw_vals, axis=-1, keepdims=True) + EPSILON)
    return (raw_vals * inverse, inverse)


def raw_gradient(grad_normed_bf, unit_vec, inverse, gain_rows):
    grad_normed = grad_normed_bf.astype(jnp.float32)
    gain_part = jnp.sum(grad_normed * unit_vec, axis=(1, 2, 3))
    grad_unit = grad_normed * gain_rows
    grad_raw = inverse * (
        grad_unit - unit_vec * jnp.mean(grad_unit * unit_vec, axis=-1, keepdims=True)
    )
    return (grad_raw.astype(jnp.bfloat16), gain_part)


def global_position(local_row, owner_index, text_rows, text_group, image_rows, grp_count):
    text_place = (
        local_row // text_group * grp_count + owner_index
    ) * text_group + local_row % text_group
    image_place = TXT + owner_index * image_rows + (local_row - text_rows)
    return jnp.where(local_row < text_rows, text_place, image_place)


def per_device(text_proj, image_proj, text_grad, image_grad, text_lengths, norm_gains):
    seq_count = lax.axis_size("seq")
    grp_count = lax.axis_size("grp")
    sample_count, head_count, image_rows, head_size = image_grad.shape
    text_group = text_proj.shape[3]
    text_rows = text_group * seq_count
    local_len = text_rows + image_rows
    text_unit, text_inverse = unit_parts(text_proj[:2])
    image_unit, image_inverse = unit_parts(image_proj[:2])
    text_gain = norm_gains[0][:, None, None, None, :]
    image_gain = norm_gains[1][:, None, None, None, :]
    text_stack = jnp.concatenate(
        [(text_unit * text_gain).astype(jnp.bfloat16), text_proj[2:]], axis=0
    )
    image_stack = jnp.concatenate(
        [(image_unit * image_gain).astype(jnp.bfloat16), image_proj[2:]], axis=0
    )
    text_here, text_cot = (
        lax.all_to_all(text_stack, "seq", split_axis=1, concat_axis=3, tiled=True),
        lax.all_to_all(text_grad[None], "seq", split_axis=1, concat_axis=3, tiled=True),
    )
    joint_rows = jnp.concatenate([text_here, image_stack], axis=3)
    cotangent_rows = jnp.concatenate([text_cot[0], image_grad], axis=2)
    key_row = jnp.arange(local_len * grp_count, dtype=jnp.int32)
    key_place = global_position(
        key_row % local_len, key_row // local_len, text_rows, text_group, image_rows, grp_count
    )
    key_valid = (key_place[None, :] >= TXT) | (key_place[None, :] < text_lengths[:, None])
    full_len = local_len * grp_count
    moved_rows, moved_cot = (
        lax.all_to_all(joint_rows, "grp", split_axis=2, concat_axis=3, tiled=True),
        lax.all_to_all(cotangent_rows[None], "grp", split_axis=2, concat_axis=3, tiled=True),
    )
    head_share = moved_rows.shape[2]
    item_count = sample_count * head_share
    flat_rows = moved_rows.reshape(3, item_count, full_len, head_size)
    item_valid = jnp.broadcast_to(
        key_valid[:, None, :], (sample_count, head_share, full_len)
    ).reshape(item_count, full_len)
    attn_local, grad_query, grad_key, grad_value = lax.map(
        whole_item,
        (
            flat_rows[0],
            flat_rows[1],
            flat_rows[2],
            item_valid,
            moved_cot.reshape(item_count, full_len, head_size),
        ),
    )
    results = jnp.stack([attn_local, grad_query, grad_key, grad_value]).reshape(
        4, sample_count, head_share, full_len, head_size
    )
    placed = lax.all_to_all(results, "grp", split_axis=3, concat_axis=2, tiled=True)
    text_back = lax.all_to_all(
        placed[:, :, :, :text_rows], "seq", split_axis=3, concat_axis=1, tiled=True
    )
    image_back = placed[:, :, :, text_rows:]
    text_raw, text_part = raw_gradient(text_back[1:3], text_unit, text_inverse, text_gain)
    image_raw, image_part = raw_gradient(image_back[1:3], image_unit, image_inverse, image_gain)
    partial_value = jnp.stack([text_part, image_part])
    summed_gain = lax.psum(partial_value, ("dp", "seq", "grp"))
    gain_grad = summed_gain / (sample_count * lax.axis_size("dp") * seq_count)
    text_proj_grad = jnp.concatenate([text_raw, text_back[3:]], axis=0)
    image_proj_grad = jnp.concatenate([image_raw, image_back[3:]], axis=0)
    return (text_back[0], image_back[0], text_proj_grad, image_proj_grad, gain_grad)


def solution(mesh):
    placed = (
        P(None, "dp", None, ("seq", "grp"), None),
        P(None, ("dp", "seq"), None, "grp", None),
        P("dp", None, ("seq", "grp"), None),
        P(("dp", "seq"), None, "grp", None),
        P(("dp", "seq")),
        P(),
    )
    return jax.shard_map(
        per_device,
        mesh=mesh,
        in_specs=placed,
        out_specs=(
            P("dp", None, ("seq", "grp"), None),
            P(("dp", "seq"), None, "grp", None),
            P(None, "dp", None, ("seq", "grp"), None),
            P(None, ("dp", "seq"), None, "grp", None),
            P(),
        ),
        check_vma=False,
    )
```

profile of v0, /device:TPU:10, one launch (start us, length us, event | category | flops | bytes accessed | tf_op | source)
XLA Modules:
  0.0 161.8 jit_solution(1333477667918705269)
XLA Ops:
  0.6 5.5 %all-to-all-start.2 = ((bf16[1,4,12,16,128]{4,3,2,0,1:T(8,128)(2,1)}), bf16[1,4,12,16,128]{4,3,2,0,1:T(8,128)(2,1)S(1)}, u32[]{:S(2)}, u32[]{:S(2)}) async-start(bf16[1,4,12,16,128]{4,3,2,0,1:T(8,128)(2,1)} %bitcast.157), calls=%async_computation.2 | async-start | bytes 393216 | tf_op jit(solution)/shard_map/all_to_all | solution.py:103
  6.8 1.3 fusion.56
  8.1 1.3 fusion.54
  12.1 4.1 %all_to_all.96 = bf16[1,1,12,144,128]{4,3,1,0,2:T(8,128)(2,1)S(1)} all-to-all(bf16[1,1,12,144,128]{4,3,1,0,2:T(8,128)(2,1)S(1)} %maximum_bitcast_fusion.1), channel_id=1, replica_groups=mesh['dp'=4,'seq'=4,'grp'=2] {'grp'}, dimensions={2} | all-to-all | bytes 884736 | tf_op jit(solution)/shard_map/all_to_all | solution.py:115
  16.2 5.0 %all-to-all-start = ((bf16[3,4,12,16,128]{4,3,2,0,1:T(8,128)(2,1)}), bf16[3,4,12,16,128]{4,3,2,0,1:T(8,128)(2,1)S(1)}, u32[]{:S(2)}, u32[]{:S(2)}) async-start(bf16[3,4,12,16,128]{4,3,2,0,1:T(8,128)(2,1)} %copy.85), calls=%async_computation | async-start | bytes 1179648 | tf_op jit(solution)/shard_map/all_to_all | solution.py:102
  23.0 11.4 %all-to-all-done = bf16[3,4,12,16,128]{4,3,2,0,1:T(8,128)(2,1)S(1)} async-done(((bf16[3,4,12,16,128]{4,3,2,0,1:T(8,128)(2,1)}), bf16[3,4,12,16,128]{4,3,2,0,1:T(8,128)(2,1)S(1)}, u32[]{:S(2)}, u32[]{:S(2)}) %all-to-all-start) | async-done | bytes 589856 | tf_op jit(solution)/shard_map/all_to_all | solution.py:102
  34.7 4.8 %all_to_all.97 = bf16[3,1,12,144,128]{4,3,1,0,2:T(8,128)(2,1)S(1)} all-to-all(bf16[3,1,12,144,128]{4,3,1,0,2:T(8,128)(2,1)S(1)} %maximum_maximum_fusion), channel_id=1, replica_groups=mesh['dp'=4,'seq'=4,'grp'=2] {'grp'}, dimensions={2} | all-to-all | bytes 2654208 | tf_op jit(solution)/shard_map/all_to_all | solution.py:114
  40.6 32.7 %while.16 = (s32[]{:T(128)}, bf16[6,288,128]{2,1,0:T(8,128)(2,1)}, bf16[6,288,128]{2,1,0:T(8,128)(2,1)}, bf16[6,288,128]{2,1,0:T(8,128)(2,1)}, bf16[6,288,128]{2...) while((s32[]{:T(128)}, bf16[6,288,128]{2,1,0:T(8,128)(2,1)}, ...), condition=%wide.region_6.7_spmd, body=%wide.region_2.6_spmd.sunk | while | flops 129290400 | bytes 4506681 | solution.py:123
  40.9 1.1 fusion.116
  43.0 1.1 multiply_reduce_fusion.2
  51.8 1.1 fusion.116
  57.3 1.1 fusion.116
  59.3 1.1 multiply_reduce_fusion.2
  62.7 1.1 fusion.116
  64.8 1.1 multiply_reduce_fusion.2
  68.2 1.1 fusion.116
  73.3 1.5 maximum_bitcast_fusion
  74.8 1.4 copy.95
  76.1 5.2 %all_to_all.98 = bf16[4,1,6,288,128]{4,0,2,1,3:T(4,128)(2,1)S(1)} all-to-all(bf16[4,1,6,288,128]{4,0,2,1,3:T(4,128)(2,1)S(1)} %copy.95), channel_id=1, replica_groups=mesh['dp'=4,'seq'=4,'grp'=2] {'grp'}, dimensions={3} | all-to-all | bytes 3538944 | tf_op jit(solution)/shard_map/all_to_all | solution.py:136
  81.7 1.6 copy.97
  83.3 7.5 %all-to-all-start.5 = ((bf16[4,1,12,64,128]{4,2,1,0,3:T(8,128)(2,1)}), bf16[4,1,12,64,128]{4,2,1,0,3:T(8,128)(2,1)}, u32[]{:S(2)}, u32[]{:S(2)}) async-start(bf16[4,1,12,64,128]{4,2,1,0,3:T(8,128)(2,1)} %copy.97), calls=%async_computation.5 | async-start | bytes 2097152 | tf_op jit(solution)/shard_map/all_to_all | solution.py:137
  94.0 19.8 %all-to-all-done.5 = bf16[4,1,12,64,128]{4,2,1,0,3:T(8,128)(2,1)} async-done(((bf16[4,1,12,64,128]{4,2,1,0,3:T(8,128)(2,1)}), bf16[4,1,12,64,128]{4,2,1,0,3:T(8,128)(2,1)}, u32[]{:S(2)}, u32[]{:S(2)}) %all-to-all-start.5) | async-done | bytes 786464 | tf_op jit(solution)/shard_map/all_to_all | solution.py:137
  113.8 1.7 %copy.98 = bf16[4,1,12,64,128]{4,3,2,0,1:T(8,128)(2,1)S(1)} copy(bf16[4,1,12,64,128]{4,2,1,0,3:T(8,128)(2,1)} %all-to-all-done.5) | data formatting | bytes 1572864 | tf_op jit(solution)/shard_map/all_to_all | solution.py:137
  116.1 42.8 %psum.7 = f32[2,2,128]{2,1,0:T(2,128)S(1)} all-reduce(f32[2,2,128]{2,1,0:T(2,128)S(1)} %pad_maximum_fusion.3), channel_id=1, replica_groups=mesh['dp'=4,'seq'=4,'grp'=2] {'dp','seq','grp'}, use_global_device_ids=true, to_apply=%region_11.12 | all-reduce | flops 512 | bytes 4096 | tf_op jit(solution)/shard_map/psum | solution.py:144
  (95 shorter events, 36.3 us)
Async XLA Ops:
  0.6 9.5 %copy-start.1 = (bf16[3,4,12,16,128]{4,3,2,1,0:T(8,128)(2,1)S(1)}, bf16[3,4,12,16,128]{4,3,2,1,0:T(8,128)(2,1)}, u32[]{:S(2)}) copy-start(bf16[3,4,12,16,128]{4,3,2,1,0:T(8,128)(2,1)} %param.8) | copy-start | bytes 1769476
  0.6 11.4 %all-to-all-start.2 = ((bf16[1,4,12,16,128]{4,3,2,0,1:T(8,128)(2,1)}), bf16[1,4,12,16,128]{4,3,2,0,1:T(8,128)(2,1)S(1)}, u32[]{:S(2)}, u32[]{:S(2)}) async-start(bf16[1,4,12,16,128]{4,3,2,0,1:T(8,128)(2,1)} %bitcast.157), calls=%async_computation.2 | async-start | bytes 393216 | tf_op jit(solution)/shard_map/all_to_all | solution.py:103
  8.1 4.0 %copy-start.3 = (bf16[1,12,80,128]{3,2,1,0:T(8,128)(2,1)S(1)}, bf16[1,12,80,128]{3,2,1,0:T(8,128)(2,1)}, u32[]{:S(2)}) copy-start(bf16[1,12,80,128]{3,2,1,0:T(8,128)(2,1)} %param.11) | copy-start | bytes 737284
  11.2 10.1 %copy-start = (bf16[3,1,12,80,128]{4,3,2,1,0:T(8,128)(2,1)S(1)}, bf16[3,1,12,80,128]{4,3,2,1,0:T(8,128)(2,1)}, u32[]{:S(2)}) copy-start(bf16[3,1,12,80,128]{4,3,2,1,0:T(8,128)(2,1)} %param.9) | copy-start | bytes 2211844
  16.2 18.2 %all-to-all-start = ((bf16[3,4,12,16,128]{4,3,2,0,1:T(8,128)(2,1)}), bf16[3,4,12,16,128]{4,3,2,0,1:T(8,128)(2,1)S(1)}, u32[]{:S(2)}, u32[]{:S(2)}) async-start(bf16[3,4,12,16,128]{4,3,2,0,1:T(8,128)(2,1)} %copy.85), calls=%async_computation | async-start | bytes 1179648 | tf_op jit(solution)/shard_map/all_to_all | solution.py:102
  39.5 1.0 copy-start.2
  83.3 30.5 %all-to-all-start.5 = ((bf16[4,1,12,64,128]{4,2,1,0,3:T(8,128)(2,1)}), bf16[4,1,12,64,128]{4,2,1,0,3:T(8,128)(2,1)}, u32[]{:S(2)}, u32[]{:S(2)}) async-start(bf16[4,1,12,64,128]{4,2,1,0,3:T(8,128)(2,1)} %copy.97), calls=%async_computation.5 | async-start | bytes 2097152 | tf_op jit(solution)/shard_map/all_to_all | solution.py:137
where the time goes:
time: 163 us; the launch traced here: 162 us
  blocking collectives  56.9 us (35%)
  waiting for transfers between devices  32.1 us (20%)
  matrix products  31 us (19%)
  starting transfers between devices  17.9 us (11%)
  local copies, waits for them, and re-layouts  12.2 us (7%)
  other arithmetic  9.94 us (6%)
    psum x1, blocking collectives, per_device(): summed_gain = lax.psum(partial_value, ('dp', 'seq', 'grp'))  42.8 us
    all_to_all x1, waiting for transfers between devices, per_device(): lax.all_to_all(placed[:, :, :, :text_rows], 'seq', split_axis=3, concat_a...  19.8 us
    all_to_all x1, waiting for transfers between devices, per_device(): lax.all_to_all(text_stack, 'seq', split_axis=1, concat_axis=3, tiled=True)  11.4 us
    all_to_all x1, starting transfers between devices, per_device(): lax.all_to_all(placed[:, :, :, :text_rows], 'seq', split_axis=3, concat_a...  7.47 us
    dot_general x6, matrix products, backward_terms(): jnp.einsum('nqk,nqd->nkd', rounded_probs, grad_out, preferred_element_typ...  6.74 us
    dot_general x6, matrix products, backward_terms(): jnp.einsum('nqd,nkd->nqk', grad_out, value_rows, preferred_element_type=j...  6.74 us
    dot_general x6, matrix products, forward(): jnp.einsum('nqk,nkd->nqd', rounded_probs, value_rows, preferred_element_t...  5.55 us
    all_to_all x1, starting transfers between devices, per_device(): lax.all_to_all(text_grad[None], 'seq', split_axis=1, concat_axis=3, tiled...  5.46 us
  transfers between devices with their start and end apart: 3, of which 3 were waited for; matrix products, arithmetic and copies ran while one was open for 6% of the time, Pallas kernels for 0%

commit v1 on v0

--- a/solution.py
+++ b/solution.py
@@ -134,9 +134,19 @@
         4, sample_count, head_share, full_len, head_size
     )
     placed = lax.all_to_all(results, "grp", split_axis=3, concat_axis=2, tiled=True)
-    text_back = lax.all_to_all(
-        placed[:, :, :, :text_rows], "seq", split_axis=3, concat_axis=1, tiled=True
-    )
+    x = placed[:, :, :, :text_rows]
+    ways, here = (lax.axis_size("seq"), lax.axis_index("seq"))
+    width = x.shape[3] // ways
+    shape = list(x.shape)
+    shape[3] = width
+    height = shape[1]
+    shape[1] = height * ways
+    text_back = jnp.zeros(shape, x.dtype)
+    for mask in range(ways):
+        part = lax.dynamic_slice_in_dim(x, (here ^ mask) * width, width, axis=3)
+        if mask:
+            part = lax.ppermute(part, "seq", [(d, d ^ mask) for d in range(ways)])
+        text_back = lax.dynamic_update_slice_in_dim(text_back, part, (here ^ mask) * height, axis=1)
     image_back = placed[:, :, :, text_rows:]
     text_raw, text_part = raw_gradient(text_back[1:3], text_unit, text_inverse, text_gain)
     image_raw, image_part = raw_gradient(image_back[1:3], image_unit, image_inverse, image_gain)

time: 163 us -> 154 us (0.945)
  the two profiles are of different devices: /device:TPU:10 before, /device:TPU:0 now
where the time goes in v1:
time: 154 us; the launch traced here: 152 us
  blocking collectives  56.5 us (37%)
  matrix products  32.8 us (21%)
  waiting for transfers between devices  27.7 us (18%)
  starting transfers between devices  14.4 us (9%)
  other arithmetic  11.2 us (7%)
  local copies, waits for them, and re-layouts  7.86 us (5%)
  between operations  1.66 us (1%)
    psum x1, blocking collectives, per_device(): summed_gain = lax.psum(partial_value, ('dp', 'seq', 'grp'))  42.5 us
    all_to_all x1, waiting for transfers between devices, per_device(): lax.all_to_all(text_stack, 'seq', split_axis=1, concat_axis=3, tiled=True)  14 us
    dot_general x6, matrix products, backward_terms(): jnp.einsum('nqk,nqd->nkd', rounded_probs, grad_out, preferred_element_typ...  10.5 us
    ppermute x3, waiting for transfers between devices, per_device(): part = lax.ppermute(part, 'seq', [(d, d ^ mask) for d in range(ways)])  10.5 us
    dot_general x6, matrix products, forward(): jnp.einsum('nqk,nkd->nqd', rounded_probs, value_rows, preferred_element_t...  7.07 us
    dot_general x6, matrix products, backward_terms(): jnp.einsum('nqd,nkd->nqk', grad_out, value_rows, preferred_element_type=j...  6.98 us
    all_to_all x1, starting transfers between devices, per_device(): lax.all_to_all(text_grad[None], 'seq', split_axis=1, concat_axis=3, tiled...  6.49 us
    all_to_all x1, blocking collectives, per_device(): lax.all_to_all(results, 'grp', split_axis=3, concat_axis=2, tiled=True)  5.16 us
  transfers between devices with their start and end apart: 5, of which 4 were waited for; matrix products, arithmetic and copies ran while one was open for 5% of the time, Pallas kernels for 0%

profile of v1, /device:TPU:0, one launch (start us, length us, event | category | flops | bytes accessed | tf_op | source)
XLA Modules:
  0.0 152.5 jit_solution(6028886223841880279)
XLA Ops:
  0.6 6.5 %all-to-all-start.2 = ((bf16[1,4,12,16,128]{4,3,2,0,1:T(8,128)(2,1)}), bf16[1,4,12,16,128]{4,3,2,0,1:T(8,128)(2,1)S(1)}, u32[]{:S(2)}, u32[]{:S(2)}) async-start(bf16[1,4,12,16,128]{4,3,2,0,1:T(8,128)(2,1)} %bitcast.147), calls=%async_computation.2 | async-start | bytes 393216 | tf_op jit(solution)/shard_map/all_to_all | solution.py:103
  7.9 1.3 fusion.56
  9.2 1.3 fusion.54
  11.4 3.3 %all-to-all-done.2 = bf16[1,4,12,16,128]{4,3,2,0,1:T(8,128)(2,1)S(1)} async-done(((bf16[1,4,12,16,128]{4,3,2,0,1:T(8,128)(2,1)}), bf16[1,4,12,16,128]{4,3,2,0,1:T(8,128)(2,1)S(1)}, u32[]{:S(2)}, u32[]{:S(2)}) %all-to-all-start.2) | async-done | bytes 196640 | tf_op jit(solution)/shard_map/all_to_all | solution.py:103
  14.7 4.1 %all_to_all.81 = bf16[1,1,12,144,128]{4,3,1,0,2:T(8,128)(2,1)S(1)} all-to-all(bf16[1,1,12,144,128]{4,3,1,0,2:T(8,128)(2,1)S(1)} %maximum_bitcast_fusion.2), channel_id=1, replica_groups=mesh['dp'=4,'seq'=4,'grp'=2] {'grp'}, dimensions={2} | all-to-all | bytes 884736 | tf_op jit(solution)/shard_map/all_to_all | solution.py:115
  18.8 3.5 %all-to-all-start = ((bf16[3,4,12,16,128]{4,3,2,0,1:T(8,128)(2,1)}), bf16[3,4,12,16,128]{4,3,2,0,1:T(8,128)(2,1)S(1)}, u32[]{:S(2)}, u32[]{:S(2)}) async-start(bf16[3,4,12,16,128]{4,3,2,0,1:T(8,128)(2,1)} %pad_maximum_fusion), calls=%async_computation | async-start | bytes 1179648 | tf_op jit(solution)/shard_map/all_to_all | solution.py:102
  24.7 14.0 %all-to-all-done = bf16[3,4,12,16,128]{4,3,2,0,1:T(8,128)(2,1)S(1)} async-done(((bf16[3,4,12,16,128]{4,3,2,0,1:T(8,128)(2,1)}), bf16[3,4,12,16,128]{4,3,2,0,1:T(8,128)(2,1)S(1)}, u32[]{:S(2)}, u32[]{:S(2)}) %all-to-all-start) | async-done | bytes 589856 | tf_op jit(solution)/shard_map/all_to_all | solution.py:102
  39.1 4.8 %all_to_all.82 = bf16[3,1,12,144,128]{4,3,1,0,2:T(8,128)(2,1)S(1)} all-to-all(bf16[3,1,12,144,128]{4,3,1,0,2:T(8,128)(2,1)S(1)} %copy.76), channel_id=1, replica_groups=mesh['dp'=4,'seq'=4,'grp'=2] {'grp'}, dimensions={2} | all-to-all | bytes 2654208 | tf_op jit(solution)/shard_map/all_to_all | solution.py:114
  45.2 34.6 %while.16 = (s32[]{:T(128)}, bf16[6,288,128]{2,1,0:T(8,128)(2,1)S(1)}, bf16[6,288,128]{2,1,0:T(8,128)(2,1)S(1)}, bf16[6,288,128]{2,1,0:T(8,128)(2,1)}, bf16[6,28...) while((s32[]{:T(128)}, ...), condition=%wide.region_6.7_spmd, body=%wide.region_2.6_spmd.sunk | while | flops 129290400 | bytes 4281905 | solution.py:123
  48.1 1.7 %fusion.109 = bf16[6,288,128]{2,1,0:T(8,128)(2,1)} fusion(bf16[6,288,128]{2,1,0:T(8,128)(2,1)} %get-tuple-element.209, s32[]{:T(128)} %get-tuple-element.205, bf16[6,288,128]{2,1,0:T(8,128)(2,1)} %get-tuple-element.225, f32[288,288]{0,1:T(8,128)S(1)} %get-tuple-element.190, f32[288]{0:T(512)S(1)} %fusion.105, f32[288]{0:T(512)S(1)} %get-tuple-element.191), kind=kOutput, calls=%fused_computation.13.clone.1 | convolution fusion | flops 21519360 | bytes 482560 | tf_op jit(solution)/shard_map/while/body/eval_jaxpr/nqk,nqd->nkd/dot_general | solution.py:29
  49.8 1.2 fusion.106
  53.8 1.8 %fusion.109 = bf16[6,288,128]{2,1,0:T(8,128)(2,1)} fusion(bf16[6,288,128]{2,1,0:T(8,128)(2,1)} %get-tuple-element.209, s32[]{:T(128)} %get-tuple-element.205, bf16[6,288,128]{2,1,0:T(8,128)(2,1)} %get-tuple-element.225, f32[288,288]{0,1:T(8,128)S(1)} %get-tuple-element.190, f32[288]{0:T(512)S(1)} %fusion.105, f32[288]{0:T(512)S(1)} %get-tuple-element.191), kind=kOutput, calls=%fused_computation.13.clone.1 | convolution fusion | flops 21519360 | bytes 482560 | tf_op jit(solution)/shard_map/while/body/eval_jaxpr/nqk,nqd->nkd/dot_general | solution.py:29
  59.6 1.7 %fusion.109 = bf16[6,288,128]{2,1,0:T(8,128)(2,1)} fusion(bf16[6,288,128]{2,1,0:T(8,128)(2,1)} %get-tuple-element.209, s32[]{:T(128)} %get-tuple-element.205, bf16[6,288,128]{2,1,0:T(8,128)(2,1)} %get-tuple-element.225, f32[288,288]{0,1:T(8,128)S(1)} %get-tuple-element.190, f32[288]{0:T(512)S(1)} %fusion.105, f32[288]{0:T(512)S(1)} %get-tuple-element.191), kind=kOutput, calls=%fused_computation.13.clone.1 | convolution fusion | flops 21519360 | bytes 482560 | tf_op jit(solution)/shard_map/while/body/eval_jaxpr/nqk,nqd->nkd/dot_general | solution.py:29
  65.4 1.7 %fusion.109 = bf16[6,288,128]{2,1,0:T(8,128)(2,1)} fusion(bf16[6,288,128]{2,1,0:T(8,128)(2,1)} %get-tuple-element.209, s32[]{:T(128)} %get-tuple-element.205, bf16[6,288,128]{2,1,0:T(8,128)(2,1)} %get-tuple-element.225, f32[288,288]{0,1:T(8,128)S(1)} %get-tuple-element.190, f32[288]{0:T(512)S(1)} %fusion.105, f32[288]{0:T(512)S(1)} %get-tuple-element.191), kind=kOutput, calls=%fused_computation.13.clone.1 | convolution fusion | flops 21519360 | bytes 482560 | tf_op jit(solution)/shard_map/while/body/eval_jaxpr/nqk,nqd->nkd/dot_general | solution.py:29
  71.1 1.7 %fusion.109 = bf16[6,288,128]{2,1,0:T(8,128)(2,1)} fusion(bf16[6,288,128]{2,1,0:T(8,128)(2,1)} %get-tuple-element.209, s32[]{:T(128)} %get-tuple-element.205, bf16[6,288,128]{2,1,0:T(8,128)(2,1)} %get-tuple-element.225, f32[288,288]{0,1:T(8,128)S(1)} %get-tuple-element.190, f32[288]{0:T(512)S(1)} %fusion.105, f32[288]{0:T(512)S(1)} %get-tuple-element.191), kind=kOutput, calls=%fused_computation.13.clone.1 | convolution fusion | flops 21519360 | bytes 482560 | tf_op jit(solution)/shard_map/while/body/eval_jaxpr/nqk,nqd->nkd/dot_general | solution.py:29
  76.9 1.8 %fusion.109 = bf16[6,288,128]{2,1,0:T(8,128)(2,1)} fusion(bf16[6,288,128]{2,1,0:T(8,128)(2,1)} %get-tuple-element.209, s32[]{:T(128)} %get-tuple-element.205, bf16[6,288,128]{2,1,0:T(8,128)(2,1)} %get-tuple-element.225, f32[288,288]{0,1:T(8,128)S(1)} %get-tuple-element.190, f32[288]{0:T(512)S(1)} %fusion.105, f32[288]{0:T(512)S(1)} %get-tuple-element.191), kind=kOutput, calls=%fused_computation.13.clone.1 | convolution fusion | flops 21519360 | bytes 482560 | tf_op jit(solution)/shard_map/while/body/eval_jaxpr/nqk,nqd->nkd/dot_general | solution.py:29
  79.9 1.4 maximum_bitcast_fusion
  81.2 1.4 copy.82
  82.6 5.2 %all_to_all.83 = bf16[4,1,6,288,128]{4,0,2,1,3:T(4,128)(2,1)S(1)} all-to-all(bf16[4,1,6,288,128]{4,0,2,1,3:T(4,128)(2,1)S(1)} %copy.82), channel_id=1, replica_groups=mesh['dp'=4,'seq'=4,'grp'=2] {'grp'}, dimensions={3} | all-to-all | bytes 3538944 | tf_op jit(solution)/shard_map/all_to_all | solution.py:136
  89.4 2.0 %collective-permute-start.1 = (bf16[4,1,12,16,128]{4,3,2,0,1:T(8,128)(2,1)S(1)}, bf16[4,1,12,16,128]{4,3,2,0,1:T(8,128)(2,1)S(1)}, u32[]{:S(2)}, u32[]{:S(2)}) collective-permute-start(bf16[4,1,12,16,128]{4,3,2,0,1:T(8,128)(2,1)S(1)} %get-tuple-element.120), channel_id=1, source_target_pairs={{0,4},{2,6},{4,0},{6,2},{1,5},{3,7},{5,1},{7,3},{8,12},{10,14},{12... | collective-permute-start | bytes 589832 | tf_op jit(solution)/shard_map/ppermute | solution.py:148
  91.4 2.4 %collective-permute-start.2 = (bf16[4,1,12,16,128]{4,3,2,0,1:T(8,128)(2,1)S(1)}, bf16[4,1,12,16,128]{4,3,2,0,1:T(8,128)(2,1)S(1)}, u32[]{:S(2)}, u32[]{:S(2)}) collective-permute-start(bf16[4,1,12,16,128]{4,3,2,0,1:T(8,128)(2,1)S(1)} %get-tuple-element.119), channel_id=1, source_target_pairs={{0,6},{2,4},{4,2},{6,0},{1,7},{3,5},{5,3},{7,1},{8,14},{10,12},{12... | collective-permute-start | bytes 589832 | tf_op jit(solution)/shard_map/ppermute | solution.py:148
  96.1 3.2 %collective-permute-done = bf16[4,1,12,16,128]{4,3,2,0,1:T(8,128)(2,1)S(1)} collective-permute-done((bf16[4,1,12,16,128]{4,3,2,0,1:T(8,128)(2,1)S(1)}, bf16[4,1,12,16,128]{4,3,2,0,1:T(8,128)(2,1)S(1)}, u32[]{:S(2)}, u32[]{:S(2)}) %collective-permute-start) | collective-permute-done | bytes 196640 | tf_op jit(solution)/shard_map/ppermute | solution.py:148
  99.3 7.2 %collective-permute-done.1 = bf16[4,1,12,16,128]{4,3,2,0,1:T(8,128)(2,1)S(1)} collective-permute-done((bf16[4,1,12,16,128]{4,3,2,0,1:T(8,128)(2,1)S(1)}, bf16[4,1,12,16,128]{4,3,2,0,1:T(8,128)(2,1)S(1)}, u32[]{:S(2)}, u32[]{:S(2)}) %collective-permute-start.1) | collective-permute-done | bytes 196640 | tf_op jit(solution)/shard_map/ppermute | solution.py:148
  107.9 42.5 %psum.7 = f32[2,2,128]{2,1,0:T(2,128)S(1)} all-reduce(f32[2,2,128]{2,1,0:T(2,128)S(1)} %pad_maximum_fusion.2), channel_id=1, replica_groups=mesh['dp'=4,'seq'=4,'grp'=2] {'dp','seq','grp'}, use_global_device_ids=true, to_apply=%region_11.12 | all-reduce | flops 512 | bytes 4096 | tf_op jit(solution)/shard_map/psum | solution.py:154
  (103 shorter events, 35.0 us)
Async XLA Ops:
  0.6 9.8 %copy-start.1 = (bf16[3,4,12,16,128]{4,3,2,1,0:T(8,128)(2,1)S(1)}, bf16[3,4,12,16,128]{4,3,2,1,0:T(8,128)(2,1)}, u32[]{:S(2)}) copy-start(bf16[3,4,12,16,128]{4,3,2,1,0:T(8,128)(2,1)} %param.8) | copy-start | bytes 1769476
  0.6 14.0 %all-to-all-start.2 = ((bf16[1,4,12,16,128]{4,3,2,0,1:T(8,128)(2,1)}), bf16[1,4,12,16,128]{4,3,2,0,1:T(8,128)(2,1)S(1)}, u32[]{:S(2)}, u32[]{:S(2)}) async-start(bf16[1,4,12,16,128]{4,3,2,0,1:T(8,128)(2,1)} %bitcast.147), calls=%async_computation.2 | async-start | bytes 393216 | tf_op jit(solution)/shard_map/all_to_all | solution.py:103
  7.1 7.5 %copy-start.4 = (bf16[1,12,80,128]{3,2,1,0:T(8,128)(2,1)S(1)}, bf16[1,12,80,128]{3,2,1,0:T(8,128)(2,1)}, u32[]{:S(2)}) copy-start(bf16[1,12,80,128]{3,2,1,0:T(8,128)(2,1)} %param.11) | copy-start | bytes 737284
  11.4 11.0 %copy-start = (bf16[3,1,12,80,128]{4,3,2,1,0:T(8,128)(2,1)S(1)}, bf16[3,1,12,80,128]{4,3,2,1,0:T(8,128)(2,1)}, u32[]{:S(2)}) copy-start(bf16[3,1,12,80,128]{4,3,2,1,0:T(8,128)(2,1)} %param.9) | copy-start | bytes 2211844
  18.8 19.9 %all-to-all-start = ((bf16[3,4,12,16,128]{4,3,2,0,1:T(8,128)(2,1)}), bf16[3,4,12,16,128]{4,3,2,0,1:T(8,128)(2,1)S(1)}, u32[]{:S(2)}, u32[]{:S(2)}) async-start(bf16[3,4,12,16,128]{4,3,2,0,1:T(8,128)(2,1)} %pad_maximum_fusion), calls=%async_computation | async-start | bytes 1179648 | tf_op jit(solution)/shard_map/all_to_all | solution.py:102
  43.9 1.0 copy-start.2
  43.9 1.3 copy-start.3
  89.3 10.0 %collective-permute-start = (bf16[4,1,12,16,128]{4,3,2,0,1:T(8,128)(2,1)S(1)}, bf16[4,1,12,16,128]{4,3,2,0,1:T(8,128)(2,1)S(1)}, u32[]{:S(2)}, u32[]{:S(2)}) collective-permute-start(bf16[4,1,12,16,128]{4,3,2,0,1:T(8,128)(2,1)S(1)} %get-tuple-element.121), channel_id=1, source_target_pairs={{0,2},{2,0},{4,6},{6,4},{1,3},{3,1},{5,7},{7,5},{8,10},{10,8},{12,... | collective-permute-start | bytes 589832 | tf_op jit(solution)/shard_map/ppermute | solution.py:148
  89.4 17.2 %collective-permute-start.1 = (bf16[4,1,12,16,128]{4,3,2,0,1:T(8,128)(2,1)S(1)}, bf16[4,1,12,16,128]{4,3,2,0,1:T(8,128)(2,1)S(1)}, u32[]{:S(2)}, u32[]{:S(2)}) collective-permute-start(bf16[4,1,12,16,128]{4,3,2,0,1:T(8,128)(2,1)S(1)} %get-tuple-element.120), channel_id=1, source_target_pairs={{0,4},{2,6},{4,0},{6,2},{1,5},{3,7},{5,1},{7,3},{8,12},{10,14},{12... | collective-permute-start | bytes 589832 | tf_op jit(solution)/shard_map/ppermute | solution.py:148
  91.4 15.2 %collective-permute-start.2 = (bf16[4,1,12,16,128]{4,3,2,0,1:T(8,128)(2,1)S(1)}, bf16[4,1,12,16,128]{4,3,2,0,1:T(8,128)(2,1)S(1)}, u32[]{:S(2)}, u32[]{:S(2)}) collective-permute-start(bf16[4,1,12,16,128]{4,3,2,0,1:T(8,128)(2,1)S(1)} %get-tuple-element.119), channel_id=1, source_target_pairs={{0,6},{2,4},{4,2},{6,0},{1,7},{3,5},{5,3},{7,1},{8,14},{10,12},{12... | collective-permute-start | bytes 589832 | tf_op jit(solution)/shard_map/ppermute | solution.py:148
